TPU v7x, 32 devices: a whole 2x2x4 slice. The times are simulated.
32 devices in a mesh: row: 8 (over z, y), ta: 4 (over x, core).
Axes of the slice: x: 2, y: 2, z: 4, core: 2. Of those that a mesh axis runs over, the one named last changes fastest.
Arguments:
- hidden: bfloat16 [8, 256, 3584], P('row', None, 'ta'), may hold values from -6 to 6
- target: bfloat16 [8, 256, 3584], P('row', None, 'ta'), may hold values from -6 to 6
- w_down: bfloat16 [8, 2, 3584, 256], P('row', None, 'ta'), may hold values from -5 to 5
- w_up: bfloat16 [8, 2, 256, 3584], P('row', None, None, 'ta'), may hold values from -5 to 5
- m_down: float32 [8, 2, 3584, 256], P('row', None, 'ta'), may hold values from -9 to 9
- m_up: float32 [8, 2, 256, 3584], P('row', None, None, 'ta'), may hold values from -9 to 9
Outputs:
- avg_down: bfloat16 [2, 3584, 256], P(None, 'ta')
- avg_up: bfloat16 [2, 256, 3584], P(None, None, 'ta')
- mom_down: float32 [2, 3584, 256], P(None, 'ta')
- mom_up: float32 [2, 256, 3584], P(None, None, 'ta')
All inputs are finite; a program needn't handle non-finite values.
Results may differ from a plain program's by a relative error of at most 0.019.
Values may be sent and summed in bfloat16 or wider, within the bound.
No kernel may reach another device: no remote copies, remote signals or barrier semaphores. Data moves between devices by JAX's collectives and lax.ppermute only.
A program may use at most 128 MiB of HBM per device.

v0:
```python
import jax
import jax.numpy as jnp
from jax import lax
from jax.sharding import PartitionSpec as P

D = 3584
RANK = 256
STEPS = 4
norm_eps = 1e-06
learn_rate = 0.02
moment_decay = 0.9


def contract(matrix_a, matrix_b, dim_a, dim_b):
    return lax.dot_general(
        matrix_a, matrix_b, (((dim_a,), (dim_b,)), ((), ())), preferred_element_type=jnp.float32
    )


def silu_slope(preact):
    sigmoid_v = jax.nn.sigmoid(preact)
    return sigmoid_v * (1.0 + preact * (1.0 - sigmoid_v))


def forward_layer(hidden, weights):
    w_down, w_up = weights
    wide_rows = hidden.astype(jnp.float32)
    squares = jnp.sum(wide_rows * wide_rows, axis=1)
    partial_value = jnp.dot(hidden, w_down, preferred_element_type=jnp.float32) * D ** (-0.5)
    projected, total_sq = lax.psum((partial_value, squares), "ta")
    root_mean = jnp.sqrt(total_sq / D + norm_eps)[:, None]
    preact = projected / root_mean
    activation = jax.nn.silu(preact).astype(jnp.bfloat16)
    lifted = jnp.dot(activation, w_up, preferred_element_type=jnp.float32) * RANK ** (-0.5)
    outcome = (wide_rows + lifted).astype(jnp.bfloat16)
    return (outcome, (hidden, root_mean, preact, activation))


def backward_layer(gradient, inputs):
    stored, weights, moments = inputs
    hidden, root_mean, preact, activation = stored
    w_down, w_up = weights
    grad_low = gradient.astype(jnp.bfloat16)
    grad_up = contract(activation, grad_low, 0, 0) * RANK ** (-0.5)
    grad_act = lax.psum(
        (contract(grad_low, w_up, 1, 1) * RANK ** (-0.5)).astype(jnp.bfloat16), "ta"
    ).astype(jnp.float32)
    grad_pre = grad_act * silu_slope(preact)
    row_dot = jnp.sum(grad_pre * preact, axis=1, keepdims=True)
    grad_proj = (grad_pre / root_mean).astype(jnp.bfloat16)
    grad_down = contract(hidden, grad_proj, 0, 0) * D ** (-0.5)
    wide_rows = hidden.astype(jnp.float32)
    through = contract(grad_proj, w_down, 1, 1) * D ** (-0.5)
    gradient = gradient + through - row_dot * wide_rows / (D * root_mean * root_mean)
    moment_down = moment_decay * moments[0] + grad_down
    moment_up = moment_decay * moments[1] + grad_up
    new_down = (w_down.astype(jnp.float32) - learn_rate * moment_down).astype(jnp.bfloat16)
    new_up = (w_up.astype(jnp.float32) - learn_rate * moment_up).astype(jnp.bfloat16)
    return (gradient, (new_down, new_up, moment_down, moment_up))


def average_whole(states):
    replicas = lax.axis_size("row")
    flat_down = states[0].astype(jnp.float32).reshape(-1)
    flat_up = states[1].astype(jnp.float32).reshape(-1)
    flat_mdown = states[2].reshape(-1)
    flat_mup = states[3].reshape(-1)
    totals = (
        lax.psum_scatter(flat_down, "row", scatter_dimension=0, tiled=True),
        lax.psum_scatter(flat_up, "row", scatter_dimension=0, tiled=True),
        lax.psum_scatter(flat_mdown, "row", scatter_dimension=0, tiled=True),
        lax.psum_scatter(flat_mup, "row", scatter_dimension=0, tiled=True),
    )
    share_down = (totals[0] / replicas).astype(jnp.bfloat16)
    share_up = (totals[1] / replicas).astype(jnp.bfloat16)
    params = (
        lax.all_gather(share_down, "row", axis=0, tiled=True),
        lax.all_gather(share_up, "row", axis=0, tiled=True),
    )
    moments = (
        lax.all_gather(
            (totals[2] / replicas).astype(jnp.bfloat16), "row", axis=0, tiled=True
        ).astype(jnp.float32),
        lax.all_gather(
            (totals[3] / replicas).astype(jnp.bfloat16), "row", axis=0, tiled=True
        ).astype(jnp.float32),
    )
    return (
        params[0].reshape(states[0].shape),
        params[1].reshape(states[1].shape),
        moments[0].reshape(states[2].shape),
        moments[1].reshape(states[3].shape),
    )


def body(hidden, target, w_down, w_up, m_down, m_up):
    tokens = hidden[0]
    target_rows = target[0].astype(jnp.float32)
    states = (w_down[0], w_up[0], m_down[0], m_up[0])
    for step_index in range(STEPS):
        outcome, stored = lax.scan(forward_layer, tokens, (states[0], states[1]))
        gradient = outcome.astype(jnp.float32) - target_rows
        gradient, states = lax.scan(
            backward_layer,
            gradient,
            (stored, (states[0], states[1]), (states[2], states[3])),
            reverse=True,
        )
    states = average_whole(states)
    return (states[0], states[1], states[2], states[3])


def solution(mesh):
    placed = (
        P("row", None, "ta"),
        P("row", None, "ta"),
        P("row", None, "ta", None),
        P("row", None, None, "ta"),
        P("row", None, "ta", None),
        P("row", None, None, "ta"),
    )
    return jax.shard_map(
        body,
        mesh=mesh,
        in_specs=placed,
        out_specs=(
            P(None, "ta", None),
            P(None, None, "ta"),
            P(None, "ta", None),
            P(None, None, "ta"),
        ),
        check_vma=False,
    )
```

profile of v0, /device:TPU:0, one launch (start us, length us, event | category | flops | bytes accessed | tf_op | source)
XLA Modules:
  0.0 1070.3 jit_solution(8603271068688036088)
XLA Ops:
  11.1 83.1 %while.160 = (s32[]{:T(128)}, bf16[256,896]{1,0:T(8,128)(2,1)S(1)}, bf16[2,256,896]{2,1,0:T(8,128)(2,1)}, f32[2,256,1]{1,2,0:T(1,128)S(1)}, f32[2,256,256]{1,2,0...) while((s32[]{:T(128)}, bf16[256,896]{1,0:T(8,128)(2,1)S(1)}, ...), condition=%wide.region_4.5_spmd, body=%wide.region_0.4_spmd.sunk | while | flops 237470208 | bytes 6695077 | solution.py:101
  22.6 27.2 %all-reduce.17.cloned.1.call-done = f32[256,256]{0,1:T(8,128)} async-done(((f32[256,256]{0,1:T(8,128)}), f32[256,256]{0,1:T(8,128)}) %all-reduce.17.cloned.1.call-update) | async-done | bytes 262160 | tf_op jit(solution)/shard_map/while/body/eval_jaxpr/psum | solution.py:30
  62.9 27.1 %all-reduce.17.cloned.1.call-done = f32[256,256]{0,1:T(8,128)} async-done(((f32[256,256]{0,1:T(8,128)}), f32[256,256]{0,1:T(8,128)}) %all-reduce.17.cloned.1.call-update) | async-done | bytes 262160 | tf_op jit(solution)/shard_map/while/body/eval_jaxpr/psum | solution.py:30
  98.1 80.0 %while.161 = (s32[]{:T(128)}, f32[256,896]{1,0:T(8,128)S(1)}, bf16[2,896,256]{2,1,0:T(8,128)(2,1)}, bf16[2,256,896]{2,1,0:T(8,128)(2,1)S(1)}, f32[2,896,256]{2,1...) while((s32[]{:T(128)}, f32[256,896]{1,0:T(8,128)S(1)}, ...), condition=%wide.region_8.9_spmd, body=%wide.region_5.8_spmd.sunk | while | flops 477167872 | bytes 56243636 | solution.py:103
  103.3 29.7 %all-reduce.19.cloned.1.call-done = bf16[256,256]{0,1:T(8,128)(2,1)} async-done(((bf16[256,256]{0,1:T(8,128)(2,1)}), bf16[256,256]{0,1:T(8,128)(2,1)}) %all-reduce.19.cloned.1.call-update) | async-done | bytes 131088 | tf_op jit(solution)/shard_map/while/body/eval_jaxpr/psum | solution.py:45
  143.5 29.3 %all-reduce.19.cloned.1.call-done = bf16[256,256]{0,1:T(8,128)(2,1)} async-done(((bf16[256,256]{0,1:T(8,128)(2,1)}), bf16[256,256]{0,1:T(8,128)(2,1)}) %all-reduce.19.cloned.1.call-update) | async-done | bytes 131088 | tf_op jit(solution)/shard_map/while/body/eval_jaxpr/psum | solution.py:45
  179.2 77.3 %while.162 = (s32[]{:T(128)}, bf16[256,896]{1,0:T(8,128)(2,1)S(1)}, bf16[2,256,896]{2,1,0:T(8,128)(2,1)}, f32[2,256,1]{1,2,0:T(1,128)S(1)}, f32[2,256,256]{1,2,0...) while((s32[]{:T(128)}, bf16[256,896]{1,0:T(8,128)(2,1)S(1)}, ...), condition=%wide.region_13.14_spmd, body=%wide.region_9.13_spmd.sunk | while | flops 237470208 | bytes 6695077 | solution.py:101
  263.1 80.4 %while.163 = (s32[]{:T(128)}, f32[256,896]{1,0:T(8,128)S(1)}, bf16[2,896,256]{2,1,0:T(8,128)(2,1)}, bf16[2,256,896]{2,1,0:T(8,128)(2,1)}, f32[2,896,256]{2,1,0:T...) while((s32[]{:T(128)}, f32[256,896]{1,0:T(8,128)S(1)}, ...), condition=%wide.region_17.18_spmd, body=%wide.region_14.17_spmd.sunk | while | flops 477167872 | bytes 56243636 | solution.py:103
  267.9 30.1 %all-reduce.23.cloned.1.call-done = bf16[256,256]{0,1:T(8,128)(2,1)} async-done(((bf16[256,256]{0,1:T(8,128)(2,1)}), bf16[256,256]{0,1:T(8,128)(2,1)}) %all-reduce.23.cloned.1.call-update) | async-done | bytes 131088 | tf_op jit(solution)/shard_map/while/body/eval_jaxpr/psum | solution.py:45
  308.1 30.1 %all-reduce.23.cloned.1.call-done = bf16[256,256]{0,1:T(8,128)(2,1)} async-done(((bf16[256,256]{0,1:T(8,128)(2,1)}), bf16[256,256]{0,1:T(8,128)(2,1)}) %all-reduce.23.cloned.1.call-update) | async-done | bytes 131088 | tf_op jit(solution)/shard_map/while/body/eval_jaxpr/psum | solution.py:45
  344.5 78.8 %while.164 = (s32[]{:T(128)}, bf16[256,896]{1,0:T(8,128)(2,1)S(1)}, bf16[2,256,896]{2,1,0:T(8,128)(2,1)}, f32[2,256,1]{1,2,0:T(1,128)S(1)}, f32[2,256,256]{1,2,0...) while((s32[]{:T(128)}, bf16[256,896]{1,0:T(8,128)(2,1)S(1)}, ...), condition=%wide.region_22.23_spmd, body=%wide.region_18.22_spmd.sunk | while | flops 237470208 | bytes 10365121 | solution.py:101
  353.5 27.0 %all-reduce.25.cloned.1.call-done = f32[256,256]{0,1:T(8,128)} async-done(((f32[256,256]{0,1:T(8,128)}), f32[256,256]{0,1:T(8,128)}) %all-reduce.25.cloned.1.call-update) | async-done | bytes 262160 | tf_op jit(solution)/shard_map/while/body/eval_jaxpr/psum | solution.py:30
  428.8 80.1 %while.165 = (s32[]{:T(128)}, f32[256,896]{1,0:T(8,128)S(1)}, bf16[2,896,256]{2,1,0:T(8,128)(2,1)}, bf16[2,256,896]{2,1,0:T(8,128)(2,1)}, f32[2,896,256]{2,1,0:T...) while((s32[]{:T(128)}, f32[256,896]{1,0:T(8,128)S(1)}, ...), condition=%wide.region_26.27_spmd, body=%wide.region_23.26_spmd.sunk | while | flops 477167872 | bytes 56243636 | solution.py:103
  433.6 30.1 %all-reduce.27.cloned.1.call-done = bf16[256,256]{0,1:T(8,128)(2,1)} async-done(((bf16[256,256]{0,1:T(8,128)(2,1)}), bf16[256,256]{0,1:T(8,128)(2,1)}) %all-reduce.27.cloned.1.call-update) | async-done | bytes 131088 | tf_op jit(solution)/shard_map/while/body/eval_jaxpr/psum | solution.py:45
  473.8 29.8 %all-reduce.27.cloned.1.call-done = bf16[256,256]{0,1:T(8,128)(2,1)} async-done(((bf16[256,256]{0,1:T(8,128)(2,1)}), bf16[256,256]{0,1:T(8,128)(2,1)}) %all-reduce.27.cloned.1.call-update) | async-done | bytes 131088 | tf_op jit(solution)/shard_map/while/body/eval_jaxpr/psum | solution.py:45
  509.9 77.6 %while.166 = (s32[]{:T(128)}, bf16[256,896]{1,0:T(8,128)(2,1)S(1)}, bf16[2,256,896]{2,1,0:T(8,128)(2,1)}, f32[2,256,1]{1,2,0:T(1,128)S(1)}, f32[2,256,256]{1,2,0...) while((s32[]{:T(128)}, bf16[256,896]{1,0:T(8,128)(2,1)S(1)}, ...), condition=%wide.region_31.32_spmd, body=%wide.region_27.31_spmd.sunk | while | flops 237470208 | bytes 10365121 | solution.py:101
  593.0 80.6 %while.167 = (s32[]{:T(128)}, f32[256,896]{1,0:T(8,128)S(1)}, bf16[2,896,256]{2,1,0:T(8,128)(2,1)}, bf16[2,256,896]{2,1,0:T(8,128)(2,1)}, f32[2,896,256]{2,1,0:T...) while((s32[]{:T(128)}, f32[256,896]{1,0:T(8,128)S(1)}, ...), condition=%wide.region_35.36_spmd, body=%wide.region_32.35_spmd.sunk | while | flops 477167872 | bytes 52573592 | solution.py:103
  597.8 30.4 %all-reduce.31.cloned.1.call-done = bf16[256,256]{0,1:T(8,128)(2,1)} async-done(((bf16[256,256]{0,1:T(8,128)(2,1)}), bf16[256,256]{0,1:T(8,128)(2,1)}) %all-reduce.31.cloned.1.call-update) | async-done | bytes 131088 | tf_op jit(solution)/shard_map/while/body/eval_jaxpr/psum | solution.py:45
  638.1 30.4 %all-reduce.31.cloned.1.call-done = bf16[256,256]{0,1:T(8,128)(2,1)} async-done(((bf16[256,256]{0,1:T(8,128)(2,1)}), bf16[256,256]{0,1:T(8,128)(2,1)}) %all-reduce.31.cloned.1.call-update) | async-done | bytes 131088 | tf_op jit(solution)/shard_map/while/body/eval_jaxpr/psum | solution.py:45
  685.9 237.4 %all-reduce.15.cloned.1.call-done = (f32[458752]{0:T(1024)}, f32[458752]{0:T(1024)}, f32[458752]{0:T(1024)}, f32[458752]{0:T(1024)}) async-done(((f32[458752]{0:T(1024)}, f32[458752]{0:T(1024)}, f32[458752]{0:T(1024)}, f32[458752]{0:T(1024)}), (f32[458752]{0:T(1024)}, f32[458752]{0:T(1024)}, f32[458752]{0:T(1024)}, f32[458752]{0:T(1024)})) %all-reduce.15.cloned.1.call-update) | async-done | bytes 7340048
  924.3 32.4 %all_gather.14 = bf16[458752]{0:T(1024)(128)(2,1)S(1)} all-gather(bf16[57344]{0:T(1024)(128)(2,1)S(1)} %fusion.173), channel_id=1, replica_groups=mesh['row'=8,'ta'=4] {'row'}, dimensions={0}, use_global_device_ids=true | all-gather | bytes 1032192 | tf_op jit(solution)/shard_map/all_gather | solution.py:81
  959.1 32.4 %all_gather.15 = bf16[458752]{0:T(1024)(128)(2,1)S(1)} all-gather(bf16[57344]{0:T(1024)(128)(2,1)S(1)} %fusion.172), channel_id=1, replica_groups=mesh['row'=8,'ta'=4] {'row'}, dimensions={0}, use_global_device_ids=true | all-gather | bytes 1032192 | tf_op jit(solution)/shard_map/all_gather | solution.py:84
  994.5 32.7 %all_gather.12 = bf16[458752]{0:T(1024)(128)(2,1)S(1)} all-gather(bf16[57344]{0:T(1024)(128)(2,1)S(1)} %fusion.175), channel_id=1, replica_groups=mesh['row'=8,'ta'=4] {'row'}, dimensions={0}, use_global_device_ids=true | all-gather | bytes 1032192 | tf_op jit(solution)/shard_map/all_gather | solution.py:77
  1029.5 31.9 %all_gather.13 = bf16[458752]{0:T(1024)(128)(2,1)S(1)} all-gather(bf16[57344]{0:T(1024)(128)(2,1)S(1)} %fusion.174), channel_id=1, replica_groups=mesh['row'=8,'ta'=4] {'row'}, dimensions={0}, use_global_device_ids=true | all-gather | bytes 1032192 | tf_op jit(solution)/shard_map/all_gather | solution.py:78
  (393 shorter events, 365.3 us)
Async XLA Ops:
  11.0 83.2 %copy-start.14 = (bf16[1,256,896]{2,1,0:T(8,128)(2,1)S(1)}, bf16[1,256,896]{2,1,0:T(8,128)(2,1)}, u32[]{:S(2)}) copy-start(bf16[1,256,896]{2,1,0:T(8,128)(2,1)} %param.23) | copy-start | bytes 1376260
  11.1 38.7 %all-reduce.17.cloned.1.call-start = ((), (), s32[]{:S(2)}) async-start(), calls=%async_computation.1 | async-start | bytes 524288 | tf_op jit(solution)/shard_map/while/body/eval_jaxpr/psum | solution.py:30
  54.0 36.0 %all-reduce.17.cloned.1.call-start = ((), (), s32[]{:S(2)}) async-start(), calls=%async_computation.1 | async-start | bytes 524288 | tf_op jit(solution)/shard_map/while/body/eval_jaxpr/psum | solution.py:30
  98.1 34.9 %all-reduce.19.cloned.1.call-start = ((), (), s32[]{:S(2)}) async-start(), calls=%async_computation.2 | async-start | bytes 262144 | tf_op jit(solution)/shard_map/while/body/eval_jaxpr/psum | solution.py:45
  133.0 4.2 copy-start.40
  138.3 34.6 %all-reduce.19.cloned.1.call-start = ((), (), s32[]{:S(2)}) async-start(), calls=%async_computation.2 | async-start | bytes 262144 | tf_op jit(solution)/shard_map/while/body/eval_jaxpr/psum | solution.py:45
  179.2 35.1 %all-reduce.21.cloned.1.call-start = ((), (), s32[]{:S(2)}) async-start(), calls=%async_computation.3 | async-start | bytes 524288 | tf_op jit(solution)/shard_map/while/body/eval_jaxpr/psum | solution.py:30
  217.8 35.1 %all-reduce.21.cloned.1.call-start = ((), (), s32[]{:S(2)}) async-start(), calls=%async_computation.3 | async-start | bytes 524288 | tf_op jit(solution)/shard_map/while/body/eval_jaxpr/psum | solution.py:30
  263.1 34.9 %all-reduce.23.cloned.1.call-start = ((), (), s32[]{:S(2)}) async-start(), calls=%async_computation.4 | async-start | bytes 262144 | tf_op jit(solution)/shard_map/while/body/eval_jaxpr/psum | solution.py:45
  303.3 34.9 %all-reduce.23.cloned.1.call-start = ((), (), s32[]{:S(2)}) async-start(), calls=%async_computation.4 | async-start | bytes 262144 | tf_op jit(solution)/shard_map/while/body/eval_jaxpr/psum | solution.py:45
  344.5 78.8 %copy-start.15 = (bf16[1,256,896]{2,1,0:T(8,128)(2,1)S(1)}, bf16[1,256,896]{2,1,0:T(8,128)(2,1)}, u32[]{:S(2)}) copy-start(bf16[1,256,896]{2,1,0:T(8,128)(2,1)} %param.23) | copy-start | bytes 1376260
  344.6 36.0 %all-reduce.25.cloned.1.call-start = ((), (), s32[]{:S(2)}) async-start(), calls=%async_computation.5 | async-start | bytes 524288 | tf_op jit(solution)/shard_map/while/body/eval_jaxpr/psum | solution.py:30
  344.6 38.0 %copy-start = (bf16[2,256,896]{2,1,0:T(8,128)(2,1)S(1)}, bf16[2,256,896]{2,1,0:T(8,128)(2,1)}, u32[]{:S(2)}) copy-start(bf16[2,256,896]{2,1,0:T(8,128)(2,1)} %get-tuple-element.2377) | copy-start | bytes 2752516 | tf_op jit(solution)/shard_map/while
  384.1 35.7 %all-reduce.25.cloned.1.call-start = ((), (), s32[]{:S(2)}) async-start(), calls=%async_computation.5 | async-start | bytes 524288 | tf_op jit(solution)/shard_map/while/body/eval_jaxpr/psum | solution.py:30
  384.1 37.7 %copy-start = (bf16[2,256,896]{2,1,0:T(8,128)(2,1)S(1)}, bf16[2,256,896]{2,1,0:T(8,128)(2,1)}, u32[]{:S(2)}) copy-start(bf16[2,256,896]{2,1,0:T(8,128)(2,1)} %get-tuple-element.2377) | copy-start | bytes 2752516 | tf_op jit(solution)/shard_map/while
  428.8 34.9 %all-reduce.27.cloned.1.call-start = ((), (), s32[]{:S(2)}) async-start(), calls=%async_computation.6 | async-start | bytes 262144 | tf_op jit(solution)/shard_map/while/body/eval_jaxpr/psum | solution.py:45
  469.0 34.6 %all-reduce.27.cloned.1.call-start = ((), (), s32[]{:S(2)}) async-start(), calls=%async_computation.6 | async-start | bytes 262144 | tf_op jit(solution)/shard_map/while/body/eval_jaxpr/psum | solution.py:45
  509.9 35.5 %all-reduce.29.cloned.1.call-start = ((), (), s32[]{:S(2)}) async-start(), calls=%async_computation.7 | async-start | bytes 524288 | tf_op jit(solution)/shard_map/while/body/eval_jaxpr/psum | solution.py:30
  510.0 37.4 %copy-start.2 = (bf16[2,256,896]{2,1,0:T(8,128)(2,1)S(1)}, bf16[2,256,896]{2,1,0:T(8,128)(2,1)}, u32[]{:S(2)}) copy-start(bf16[2,256,896]{2,1,0:T(8,128)(2,1)} %get-tuple-element.2449) | copy-start | bytes 2752516 | tf_op jit(solution)/shard_map/while
  548.9 35.1 %all-reduce.29.cloned.1.call-start = ((), (), s32[]{:S(2)}) async-start(), calls=%async_computation.7 | async-start | bytes 524288 | tf_op jit(solution)/shard_map/while/body/eval_jaxpr/psum | solution.py:30
  548.9 37.1 %copy-start.2 = (bf16[2,256,896]{2,1,0:T(8,128)(2,1)S(1)}, bf16[2,256,896]{2,1,0:T(8,128)(2,1)}, u32[]{:S(2)}) copy-start(bf16[2,256,896]{2,1,0:T(8,128)(2,1)} %get-tuple-element.2449) | copy-start | bytes 2752516 | tf_op jit(solution)/shard_map/while
  593.0 35.2 %all-reduce.31.cloned.1.call-start = ((), (), s32[]{:S(2)}) async-start(), calls=%async_computation.8 | async-start | bytes 262144 | tf_op jit(solution)/shard_map/while/body/eval_jaxpr/psum | solution.py:45
  633.3 35.2 %all-reduce.31.cloned.1.call-start = ((), (), s32[]{:S(2)}) async-start(), calls=%async_computation.8 | async-start | bytes 262144 | tf_op jit(solution)/shard_map/while/body/eval_jaxpr/psum | solution.py:45
  673.6 249.7 %all-reduce.15.cloned.1.call-start = ((), (), s32[]{:S(2)}) async-start(), calls=%async_computation | async-start | bytes 14680064
  (71 other events, 130.3 us)
Sparse Core Ops, SparseCore 0:
  14.8 34.9 all-reduce.16
  57.7 32.2 all-reduce.16
  101.2 31.7 all-reduce.18
  141.1 31.7 all-reduce.18
  182.0 32.2 all-reduce.20
  220.7 32.2 all-reduce.20
  266.2 31.7 all-reduce.22
  306.4 31.7 all-reduce.22
  348.3 32.2 all-reduce.24
  387.5 32.2 all-reduce.24
  431.9 31.7 all-reduce.26
  471.7 31.7 all-reduce.26
  513.1 32.2 all-reduce.28
  551.7 32.2 all-reduce.28
  596.4 31.7 all-reduce.30
  636.7 31.7 all-reduce.30
Sparse Core Ops, SparseCore 1:
  684.2 239.1 all-reduce.14
where the time goes:
time: 1070 us
  waiting for transfers between devices  691 us (65%)
  blocking collectives  178 us (17%)
  matrix products  85.7 us (8%)
  local copies, waits for them, and re-layouts  72.1 us (7%)
  other arithmetic  26.6 us (2%)
  between operations  16.1 us (2%)
    psum x8, waiting for transfers between devices, backward_layer(): lax.psum((contract(grad_low, w_up, 1, 1) * RANK ** (-0.5)).astype(jnp.bfl...  240 us
    unnamed x2, waiting for transfers between devices  237 us
    psum x8, waiting for transfers between devices, forward_layer(): projected, total_sq = lax.psum((partial_value, squares), 'ta')  213 us
    dot_general x32, matrix products, contract(): lax.dot_general(matrix_a, matrix_b, (((dim_a,), (dim_b,)), ((), ())), pre...  57 us
    psum x8, blocking collectives, forward_layer(): projected, total_sq = lax.psum((partial_value, squares), 'ta')  48.4 us
    all_gather x1, blocking collectives, average_whole(): lax.all_gather(share_down, 'row', axis=0, tiled=True)  32.7 us
    all_gather x1, blocking collectives, average_whole(): lax.all_gather((totals[2] / replicas).astype(jnp.bfloat16), 'row', axis=0...  32.4 us
    all_gather x1, blocking collectives, average_whole(): lax.all_gather((totals[3] / replicas).astype(jnp.bfloat16), 'row', axis=0...  32.4 us
  transfers between devices with their start and end apart: 17, of which 17 were waited for; matrix products, arithmetic and copies ran while one was open for 3% of the time, Pallas kernels for 0%

commit v1 on v0

--- a/solution.py
+++ b/solution.py
@@ -42,8 +42,11 @@
     w_down, w_up = weights
     grad_low = gradient.astype(jnp.bfloat16)
     grad_up = contract(activation, grad_low, 0, 0) * RANK ** (-0.5)
-    grad_act = lax.psum(
-        (contract(grad_low, w_up, 1, 1) * RANK ** (-0.5)).astype(jnp.bfloat16), "ta"
+    grad_act = jnp.sum(
+        lax.all_gather(
+            (contract(grad_low, w_up, 1, 1) * RANK ** (-0.5)).astype(jnp.bfloat16), "ta"
+        ),
+        axis=0,
     ).astype(jnp.float32)
     grad_pre = grad_act * silu_slope(preact)
     row_dot = jnp.sum(grad_pre * preact, axis=1, keepdims=True)

time: 1070 us -> 906 us (0.85)
  waiting for transfers between devices: 691 us -> 450 us
  blocking collectives: 178 us -> 237 us
  local copies, waits for them, and re-layouts: 72.1 us -> 96.8 us
  matrix products: 85.7 us -> 67.2 us
    psum x8 -> x0, waiting for transfers between devices: 240 us -> none  [backward_layer(): lax.psum((contract(grad_low, w_up, 1, 1) * RANK ** (-0.5)).astype(jnp.bfl...]
    all_gather x0 -> x8, blocking collectives: none -> 56 us  [backward_layer(): lax.all_gather((contract(grad_low, w_up, 1, 1) * RANK ** (-0.5)).astype(j...]
    while x132 -> x192, local copies, waits for them, and re-layouts: 21.4 us -> 41.3 us
    dot_general x32, matrix products: 57 us -> 38.4 us  [contract(): lax.dot_general(matrix_a, matrix_b, (((dim_a,), (dim_b,)), ((), ())), pre...]
  transfers between devices with their start and end apart: 17 -> 9, of which waited for: 17 -> 9; matrix products, arithmetic and copies ran while one was open for 3% -> 1% of each run, Pallas kernels for 0% -> 0%
where the time goes in v1:
time: 906 us; the launch traced here: 904 us
  waiting for transfers between devices  450 us (50%)
  blocking collectives  237 us (26%)
  local copies, waits for them, and re-layouts  96.8 us (11%)
  matrix products  67.2 us (7%)
  other arithmetic  33.6 us (4%)
  between operations  16.4 us (2%)
    unnamed x2, waiting for transfers between devices  238 us
    psum x8, waiting for transfers between devices, forward_layer(): projected, total_sq = lax.psum((partial_value, squares), 'ta')  212 us
    all_gather x8, blocking collectives, backward_layer(): lax.all_gather((contract(grad_low, w_up, 1, 1) * RANK ** (-0.5)).astype(j...  56 us
    psum x8, blocking collectives, forward_layer(): projected, total_sq = lax.psum((partial_value, squares), 'ta')  51.6 us
    while x192, local copies, waits for them, and re-layouts  41.3 us
    dot_general x32, matrix products, contract(): lax.dot_general(matrix_a, matrix_b, (((dim_a,), (dim_b,)), ((), ())), pre...  38.4 us
    all_gather x1, blocking collectives, average_whole(): lax.all_gather(share_down, 'row', axis=0, tiled=True)  32.7 us
    all_gather x1, blocking collectives, average_whole(): lax.all_gather((totals[2] / replicas).astype(jnp.bfloat16), 'row', axis=0...  32.4 us
  transfers between devices with their start and end apart: 9, of which 9 were waited for; matrix products, arithmetic and copies ran while one was open for 1% of the time, Pallas kernels for 0%

profile of v1, /device:TPU:0, one launch (start us, length us, event | category | flops | bytes accessed | tf_op | source)
XLA Modules:
  0.0 903.5 jit_solution(3164992369464395191)
XLA Ops:
  11.0 83.1 %while.160 = (s32[]{:T(128)}, bf16[256,896]{1,0:T(8,128)(2,1)S(1)}, bf16[2,256,896]{2,1,0:T(8,128)(2,1)}, f32[2,256,1]{1,2,0:T(1,128)S(1)}, f32[2,256,256]{1,2,0...) while((s32[]{:T(128)}, bf16[256,896]{1,0:T(8,128)(2,1)S(1)}, ...), condition=%wide.region_4.5_spmd, body=%wide.region_0.4_spmd.sunk | while | flops 237470208 | bytes 6695077 | solution.py:104
  14.2 8.3 psum.65
  22.6 27.2 %all-reduce.13.cloned.1.call-done = f32[256,256]{0,1:T(8,128)} async-done(((f32[256,256]{0,1:T(8,128)}), f32[256,256]{0,1:T(8,128)}) %all-reduce.13.cloned.1.call-update) | async-done | bytes 262160 | tf_op jit(solution)/shard_map/while/body/eval_jaxpr/psum | solution.py:30
  62.8 27.1 %all-reduce.13.cloned.1.call-done = f32[256,256]{0,1:T(8,128)} async-done(((f32[256,256]{0,1:T(8,128)}), f32[256,256]{0,1:T(8,128)}) %all-reduce.13.cloned.1.call-update) | async-done | bytes 262160 | tf_op jit(solution)/shard_map/while/body/eval_jaxpr/psum | solution.py:30
  99.0 40.9 %while.161 = (s32[]{:T(128)}, f32[256,896]{1,0:T(8,128)S(1)}, bf16[2,896,256]{2,1,0:T(8,128)(2,1)}, bf16[2,256,896]{2,1,0:T(8,128)(2,1)}, f32[2,896,256]{2,1,0:T...) while((s32[]{:T(128)}, f32[256,896]{1,0:T(8,128)S(1)}, ...), condition=%wide.region_8.9_spmd, body=%wide.region_5.8_spmd.sunk | while | flops 477298944 | bytes 75642352 | solution.py:106
  120.4 7.7 all-gather.8
  141.0 78.3 %while.162 = (s32[]{:T(128)}, bf16[256,896]{1,0:T(8,128)(2,1)S(1)}, bf16[2,256,896]{2,1,0:T(8,128)(2,1)}, f32[2,256,1]{1,2,0:T(1,128)S(1)}, f32[2,256,256]{1,2,0...) while((s32[]{:T(128)}, bf16[256,896]{1,0:T(8,128)(2,1)S(1)}, ...), condition=%wide.region_13.14_spmd, body=%wide.region_9.13_spmd.sunk | while | flops 237470208 | bytes 10365121 | solution.py:104
  151.1 26.1 %all-reduce.15.cloned.1.call-done = f32[256,256]{0,1:T(8,128)} async-done(((f32[256,256]{0,1:T(8,128)}), f32[256,256]{0,1:T(8,128)}) %all-reduce.15.cloned.1.call-update) | async-done | bytes 262160 | tf_op jit(solution)/shard_map/while/body/eval_jaxpr/psum | solution.py:30
  189.6 26.2 %all-reduce.15.cloned.1.call-done = f32[256,256]{0,1:T(8,128)} async-done(((f32[256,256]{0,1:T(8,128)}), f32[256,256]{0,1:T(8,128)}) %all-reduce.15.cloned.1.call-update) | async-done | bytes 262160 | tf_op jit(solution)/shard_map/while/body/eval_jaxpr/psum | solution.py:30
  224.8 37.3 %while.163 = (s32[]{:T(128)}, f32[256,896]{1,0:T(8,128)S(1)}, bf16[2,896,256]{2,1,0:T(8,128)(2,1)}, bf16[2,256,896]{2,1,0:T(8,128)(2,1)}, f32[2,896,256]{2,1,0:T...) while((s32[]{:T(128)}, f32[256,896]{1,0:T(8,128)S(1)}, ...), condition=%wide.region_17.18_spmd, body=%wide.region_14.17_spmd.sunk | while | flops 477298944 | bytes 77739560 | solution.py:106
  263.2 79.3 %while.164 = (s32[]{:T(128)}, bf16[256,896]{1,0:T(8,128)(2,1)S(1)}, bf16[2,256,896]{2,1,0:T(8,128)(2,1)}, f32[2,256,1]{1,2,0:T(1,128)S(1)}, f32[2,256,256]{1,2,0...) while((s32[]{:T(128)}, bf16[256,896]{1,0:T(8,128)(2,1)S(1)}, ...), condition=%wide.region_22.23_spmd, body=%wide.region_18.22_spmd.sunk | while | flops 237470208 | bytes 10365121 | solution.py:104
  273.4 26.4 %all-reduce.17.cloned.1.call-done = f32[256,256]{0,1:T(8,128)} async-done(((f32[256,256]{0,1:T(8,128)}), f32[256,256]{0,1:T(8,128)}) %all-reduce.17.cloned.1.call-update) | async-done | bytes 262160 | tf_op jit(solution)/shard_map/while/body/eval_jaxpr/psum | solution.py:30
  312.3 26.7 %all-reduce.17.cloned.1.call-done = f32[256,256]{0,1:T(8,128)} async-done(((f32[256,256]{0,1:T(8,128)}), f32[256,256]{0,1:T(8,128)}) %all-reduce.17.cloned.1.call-update) | async-done | bytes 262160 | tf_op jit(solution)/shard_map/while/body/eval_jaxpr/psum | solution.py:30
  347.9 35.7 %while.165 = (s32[]{:T(128)}, f32[256,896]{1,0:T(8,128)S(1)}, bf16[2,896,256]{2,1,0:T(8,128)(2,1)}, bf16[2,256,896]{2,1,0:T(8,128)(2,1)}, f32[2,896,256]{2,1,0:T...) while((s32[]{:T(128)}, f32[256,896]{1,0:T(8,128)S(1)}, ...), condition=%wide.region_26.27_spmd, body=%wide.region_23.26_spmd.sunk | while | flops 477298944 | bytes 73545176 | solution.py:106
  384.7 78.6 %while.166 = (s32[]{:T(128)}, bf16[256,896]{1,0:T(8,128)(2,1)S(1)}, bf16[2,256,896]{2,1,0:T(8,128)(2,1)}, f32[2,256,1]{1,2,0:T(1,128)S(1)}, f32[2,256,256]{1,2,0...) while((s32[]{:T(128)}, bf16[256,896]{1,0:T(8,128)(2,1)S(1)}, ...), condition=%wide.region_31.32_spmd, body=%wide.region_27.31_spmd.sunk | while | flops 237470208 | bytes 10365121 | solution.py:104
  394.7 26.1 %all-reduce.19.cloned.1.call-done = f32[256,256]{0,1:T(8,128)} async-done(((f32[256,256]{0,1:T(8,128)}), f32[256,256]{0,1:T(8,128)}) %all-reduce.19.cloned.1.call-update) | async-done | bytes 262160 | tf_op jit(solution)/shard_map/while/body/eval_jaxpr/psum | solution.py:30
  433.2 26.5 %all-reduce.19.cloned.1.call-done = f32[256,256]{0,1:T(8,128)} async-done(((f32[256,256]{0,1:T(8,128)}), f32[256,256]{0,1:T(8,128)}) %all-reduce.19.cloned.1.call-update) | async-done | bytes 262160 | tf_op jit(solution)/shard_map/while/body/eval_jaxpr/psum | solution.py:30
  468.8 38.2 %while.167 = (s32[]{:T(128)}, f32[256,896]{1,0:T(8,128)S(1)}, bf16[2,896,256]{2,1,0:T(8,128)(2,1)}, bf16[2,256,896]{2,1,0:T(8,128)(2,1)}, f32[2,896,256]{2,1,0:T...) while((s32[]{:T(128)}, f32[256,896]{1,0:T(8,128)S(1)}, ...), condition=%wide.region_35.36_spmd, body=%wide.region_32.35_spmd.sunk | while | flops 477298944 | bytes 74069488 | solution.py:106
  488.6 7.3 all-gather.11
  518.2 238.0 %all-reduce.11.cloned.1.call-done = (f32[458752]{0:T(1024)}, f32[458752]{0:T(1024)}, f32[458752]{0:T(1024)}, f32[458752]{0:T(1024)}) async-done(((f32[458752]{0:T(1024)}, f32[458752]{0:T(1024)}, f32[458752]{0:T(1024)}, f32[458752]{0:T(1024)}), (f32[458752]{0:T(1024)}, f32[458752]{0:T(1024)}, f32[458752]{0:T(1024)}, f32[458752]{0:T(1024)})) %all-reduce.11.cloned.1.call-update) | async-done | bytes 7340048
  757.2 32.4 %all_gather.86 = bf16[458752]{0:T(1024)(128)(2,1)S(1)} all-gather(bf16[57344]{0:T(1024)(128)(2,1)S(1)} %fusion.193), channel_id=1, replica_groups=mesh['row'=8,'ta'=4] {'row'}, dimensions={0}, use_global_device_ids=true | all-gather | bytes 1032192 | tf_op jit(solution)/shard_map/all_gather | solution.py:84
  792.0 32.4 %all_gather.87 = bf16[458752]{0:T(1024)(128)(2,1)S(1)} all-gather(bf16[57344]{0:T(1024)(128)(2,1)S(1)} %fusion.192), channel_id=1, replica_groups=mesh['row'=8,'ta'=4] {'row'}, dimensions={0}, use_global_device_ids=true | all-gather | bytes 1032192 | tf_op jit(solution)/shard_map/all_gather | solution.py:87
  827.4 32.7 %all_gather.84 = bf16[458752]{0:T(1024)(128)(2,1)S(1)} all-gather(bf16[57344]{0:T(1024)(128)(2,1)S(1)} %fusion.195), channel_id=1, replica_groups=mesh['row'=8,'ta'=4] {'row'}, dimensions={0}, use_global_device_ids=true | all-gather | bytes 1032192 | tf_op jit(solution)/shard_map/all_gather | solution.py:80
  862.4 31.9 %all_gather.85 = bf16[458752]{0:T(1024)(128)(2,1)S(1)} all-gather(bf16[57344]{0:T(1024)(128)(2,1)S(1)} %fusion.194), channel_id=1, replica_groups=mesh['row'=8,'ta'=4] {'row'}, dimensions={0}, use_global_device_ids=true | all-gather | bytes 1032192 | tf_op jit(solution)/shard_map/all_gather | solution.py:81
  (463 shorter events, 282.4 us)
Async XLA Ops:
  11.0 83.2 %copy-start.29 = (bf16[1,256,896]{2,1,0:T(8,128)(2,1)S(1)}, bf16[1,256,896]{2,1,0:T(8,128)(2,1)}, u32[]{:S(2)}) copy-start(bf16[1,256,896]{2,1,0:T(8,128)(2,1)} %param.23) | copy-start | bytes 1376260
  11.0 38.7 %all-reduce.13.cloned.1.call-start = ((), (), s32[]{:S(2)}) async-start(), calls=%async_computation.1 | async-start | bytes 524288 | tf_op jit(solution)/shard_map/while/body/eval_jaxpr/psum | solution.py:30
  54.0 36.0 %all-reduce.13.cloned.1.call-start = ((), (), s32[]{:S(2)}) async-start(), calls=%async_computation.1 | async-start | bytes 524288 | tf_op jit(solution)/shard_map/while/body/eval_jaxpr/psum | solution.py:30
  109.5 4.3 copy-start.25
  130.3 4.3 copy-start.25
  141.0 78.3 %copy-start.30 = (bf16[1,256,896]{2,1,0:T(8,128)(2,1)S(1)}, bf16[1,256,896]{2,1,0:T(8,128)(2,1)}, u32[]{:S(2)}) copy-start(bf16[1,256,896]{2,1,0:T(8,128)(2,1)} %param.23) | copy-start | bytes 1376260
  141.0 36.1 %all-reduce.15.cloned.1.call-start = ((), (), s32[]{:S(2)}) async-start(), calls=%async_computation.2 | async-start | bytes 524288 | tf_op jit(solution)/shard_map/while/body/eval_jaxpr/psum | solution.py:30
  141.0 38.1 %copy-start.2 = (bf16[2,256,896]{2,1,0:T(8,128)(2,1)S(1)}, bf16[2,256,896]{2,1,0:T(8,128)(2,1)}, u32[]{:S(2)}) copy-start(bf16[2,256,896]{2,1,0:T(8,128)(2,1)} %get-tuple-element.2312) | copy-start | bytes 2752516 | tf_op jit(solution)/shard_map/while
  180.6 35.1 %all-reduce.15.cloned.1.call-start = ((), (), s32[]{:S(2)}) async-start(), calls=%async_computation.2 | async-start | bytes 524288 | tf_op jit(solution)/shard_map/while/body/eval_jaxpr/psum | solution.py:30
  180.7 37.1 %copy-start.2 = (bf16[2,256,896]{2,1,0:T(8,128)(2,1)S(1)}, bf16[2,256,896]{2,1,0:T(8,128)(2,1)}, u32[]{:S(2)}) copy-start(bf16[2,256,896]{2,1,0:T(8,128)(2,1)} %get-tuple-element.2312) | copy-start | bytes 2752516 | tf_op jit(solution)/shard_map/while
  263.2 79.3 %copy-start.31 = (bf16[1,256,896]{2,1,0:T(8,128)(2,1)S(1)}, bf16[1,256,896]{2,1,0:T(8,128)(2,1)}, u32[]{:S(2)}) copy-start(bf16[1,256,896]{2,1,0:T(8,128)(2,1)} %param.23) | copy-start | bytes 1376260
  263.4 36.4 %all-reduce.17.cloned.1.call-start = ((), (), s32[]{:S(2)}) async-start(), calls=%async_computation.3 | async-start | bytes 524288 | tf_op jit(solution)/shard_map/while/body/eval_jaxpr/psum | solution.py:30
  263.4 38.4 %copy-start.7 = (bf16[2,256,896]{2,1,0:T(8,128)(2,1)S(1)}, bf16[2,256,896]{2,1,0:T(8,128)(2,1)}, u32[]{:S(2)}) copy-start(bf16[2,256,896]{2,1,0:T(8,128)(2,1)} %get-tuple-element.2387) | copy-start | bytes 2752516 | tf_op jit(solution)/shard_map/while
  303.3 35.7 %all-reduce.17.cloned.1.call-start = ((), (), s32[]{:S(2)}) async-start(), calls=%async_computation.3 | async-start | bytes 524288 | tf_op jit(solution)/shard_map/while/body/eval_jaxpr/psum | solution.py:30
  303.3 37.7 %copy-start.7 = (bf16[2,256,896]{2,1,0:T(8,128)(2,1)S(1)}, bf16[2,256,896]{2,1,0:T(8,128)(2,1)}, u32[]{:S(2)}) copy-start(bf16[2,256,896]{2,1,0:T(8,128)(2,1)} %get-tuple-element.2387) | copy-start | bytes 2752516 | tf_op jit(solution)/shard_map/while
  374.1 4.2 copy-start.21
  384.7 79.3 %copy-start.32 = (bf16[1,256,896]{2,1,0:T(8,128)(2,1)S(1)}, bf16[1,256,896]{2,1,0:T(8,128)(2,1)}, u32[]{:S(2)}) copy-start(bf16[1,256,896]{2,1,0:T(8,128)(2,1)} %param.23) | copy-start | bytes 1376260
  384.7 36.1 %all-reduce.19.cloned.1.call-start = ((), (), s32[]{:S(2)}) async-start(), calls=%async_computation.4 | async-start | bytes 524288 | tf_op jit(solution)/shard_map/while/body/eval_jaxpr/psum | solution.py:30
  384.7 38.1 %copy-start.12 = (bf16[2,256,896]{2,1,0:T(8,128)(2,1)S(1)}, bf16[2,256,896]{2,1,0:T(8,128)(2,1)}, u32[]{:S(2)}) copy-start(bf16[2,256,896]{2,1,0:T(8,128)(2,1)} %get-tuple-element.2462) | copy-start | bytes 2752516 | tf_op jit(solution)/shard_map/while
  424.3 35.5 %all-reduce.19.cloned.1.call-start = ((), (), s32[]{:S(2)}) async-start(), calls=%async_computation.4 | async-start | bytes 524288 | tf_op jit(solution)/shard_map/while/body/eval_jaxpr/psum | solution.py:30
  424.3 37.4 %copy-start.12 = (bf16[2,256,896]{2,1,0:T(8,128)(2,1)S(1)}, bf16[2,256,896]{2,1,0:T(8,128)(2,1)}, u32[]{:S(2)}) copy-start(bf16[2,256,896]{2,1,0:T(8,128)(2,1)} %get-tuple-element.2462) | copy-start | bytes 2752516 | tf_op jit(solution)/shard_map/while
  463.2 293.0 %all-reduce.11.cloned.1.call-start = ((), (), s32[]{:S(2)}) async-start(), calls=%async_computation | async-start | bytes 14680064
  477.5 4.5 copy-start.45
  497.0 4.4 copy-start.45
  (98 other events, 189.2 us)
Sparse Core Ops, SparseCore 0:
  14.8 34.9 all-reduce.12
  57.7 32.2 all-reduce.12
  144.1 32.9 all-reduce.14
  183.5 32.2 all-reduce.14
  266.8 32.9 all-reduce.16
  306.7 32.2 all-reduce.16
  387.8 32.8 all-reduce.18
  427.4 32.2 all-reduce.18
Sparse Core Ops, SparseCore 1:
  516.4 239.7 all-reduce.10
